TPU v7x, 256 devices: a whole 4x4x8 slice. The times are simulated.
256 devices in a mesh: patch: 32 (over z, y), seq: 4 (over x), req: 2 (over core).
Axes of the slice: x: 4, y: 4, z: 8, core: 2. Of those that a mesh axis runs over, the one named last changes fastest.
Arguments:
- query: bfloat16 [4, 64, 3584], P(None, ('patch', 'req')), may hold values from -20 to 20
- text_cache: bfloat16 [4, 64, 3072, 1024], P(None, ('patch', 'req'), 'seq'), may hold values from -6 to 6
- text_len: int32 [64], P(('patch', 'req')), may hold values from 0 to 3072
- image_rows: bfloat16 [4, 65536, 1024], P(None, ('patch', 'seq', 'req')), may hold values from -6 to 6
- patch_map: int32 [65536], P(('patch', 'seq', 'req')), may hold values from 0 to 63, as said below
- image_places: int32 [65536], P(('patch', 'seq', 'req')), may hold values from 0 to 1023, as said below
Outputs:
- attended: bfloat16 [4, 64, 3584], P(None, ('patch', 'req'), 'seq')
- image_cache: bfloat16 [4, 64, 1024, 1024], P(None, ('patch', 'req'), 'seq')
Inputs may be any that keep to these rules, and one draw needn't show every extreme that they name: `patch_map`: each aligned block of 256 rows (the rows of one prefill device) holds exactly 4 rows of every request. `image_places`: together with patch_map every pair of request and position occurs exactly once. The rows of a device whose seq index is s have positions from s * 256 to (s + 1) * 256 - 1.
All inputs are finite; a program needn't handle non-finite values.
Results may differ from a plain program's by a relative error of at most 0.0026.
Values may be sent and summed in bfloat16 or wider, within the bound.
A program may use at most 64 MiB of HBM per device.

v0:
```python
import math

import jax
import jax.numpy as jnp
from jax import lax
from jax.sharding import PartitionSpec as P

HEADS = 28
KV_HEADS = 4
HEAD_DIM = 128


def copy_for_each(x, axis):
    copies = jnp.broadcast_to(x, (lax.axis_size(axis), *x.shape))
    return lax.all_to_all(copies, axis, split_axis=0, concat_axis=0, tiled=True)


def gathered_once(x, axis):
    leaves = jax.tree.leaves(x)
    turns = sorted(range(len(leaves)), key=lambda k: -leaves[k].size)
    width = (1, *leaves[turns[0]].shape)[-1]
    lines = [
        jnp.pad(leaves[k].reshape(-1), (0, -leaves[k].size % width)).reshape(-1, width)
        for k in turns
    ]
    both, at, found = (copy_for_each(jnp.concatenate(lines), axis), 0, {})
    for k, line in zip(turns, lines):
        piece = both[:, at : at + len(line)].reshape(len(both), -1)
        found[k] = piece[:, : leaves[k].size].reshape(-1, *leaves[k].shape)
        at += len(line)
    numbers = iter(range(len(leaves)))
    return jax.tree.map(lambda _: found[next(numbers)], x)


def folded_in_pairs(pieces, combine):
    while len(jax.tree.leaves(pieces)[0]) > 1:
        pieces = jax.vmap(combine)(
            *(jax.tree.map(lambda part: part[side::2], pieces) for side in (0, 1))
        )
    return jax.tree.map(lambda part: part[0], pieces)


def combined_all(x, axis, combine):
    pieces = gathered_once(x, axis)
    return folded_in_pairs(pieces, combine)


def merge_partials(first, second):
    top = jnp.maximum(first[0], second[0])
    left = jnp.exp(first[0] - top)
    right = jnp.exp(second[0] - top)
    total = left * first[1] + right * second[1]
    values = left[..., None] * first[2] + right[..., None] * second[2]
    return (top, total, values)


def body(query, text_cache, text_len, image_rows, patch_map, image_places):
    layers, req_dev, query_width = query.shape
    text_dev = text_cache.shape[2]
    full_width = text_cache.shape[3]
    kv_width = full_width // 2
    head_dim = HEAD_DIM
    kv_heads = KV_HEADS
    heads = HEADS
    group = heads // kv_heads
    src_rows = image_rows.shape[1]
    patch_count = lax.axis_size("patch")
    req_count = lax.axis_size("req")
    seq_count = lax.axis_size("seq")
    seq_index = lax.axis_index("seq")
    per_source = src_rows // (patch_count * req_count * req_dev)
    band_size = per_source * patch_count * req_count
    scale = 1.0 / math.sqrt(head_dim)
    order = jnp.argsort(patch_map, stable=True)
    grouped = jnp.take(image_rows, order, axis=1)
    grouped_places = jnp.take(image_places, order)
    sending = grouped.reshape(layers, patch_count * req_count, req_dev, per_source, full_width)
    arrived = lax.all_to_all(sending, ("patch", "req"), split_axis=1, concat_axis=3, tiled=True)
    place_send = grouped_places.reshape(patch_count * req_count, req_dev, per_source)
    arrived_places = lax.all_to_all(
        place_send, ("patch", "req"), split_axis=0, concat_axis=2, tiled=True
    )
    image_block = arrived.reshape(layers, req_dev, band_size, full_width)
    local_places = arrived_places.reshape(req_dev, band_size) - seq_index * band_size
    inverse = jnp.argsort(local_places, axis=1)
    image_cache = jnp.take_along_axis(image_block, inverse[None, :, :, None], axis=2)
    queries = query.reshape(layers, req_dev, kv_heads, group, head_dim)
    text_keys = text_cache[..., :kv_width].reshape(layers, req_dev, text_dev, kv_heads, head_dim)
    text_values = text_cache[..., kv_width:].reshape(layers, req_dev, text_dev, kv_heads, head_dim)
    image_keys = image_block[..., :kv_width].reshape(layers, req_dev, band_size, kv_heads, head_dim)
    image_values = image_block[..., kv_width:].reshape(
        layers, req_dev, band_size, kv_heads, head_dim
    )
    positions = seq_index * text_dev + jnp.arange(text_dev, dtype=jnp.int32)
    used = positions[None, :] < text_len[:, None]
    block = min(256, text_dev)
    live_len = jnp.max(jnp.clip(text_len - seq_index * text_dev, 0, text_dev))
    live_blocks = (live_len + block - 1) // block

    def fill(index, buffer):
        start = index * block
        keys_block = lax.dynamic_slice_in_dim(text_keys, start, block, 2)
        raw = (
            jnp.einsum(
                "lrkgd,lrtkd->lrkgt", queries, keys_block, preferred_element_type=jnp.float32
            )
            * scale
        )
        usable = lax.dynamic_slice_in_dim(used, start, block, 1)
        masked = jnp.where(usable[None, :, None, None, :], raw, -jnp.inf)
        return lax.dynamic_update_slice_in_dim(buffer, masked, start, 4)

    empty = jnp.full((layers, req_dev, kv_heads, group, text_dev), -jnp.inf, jnp.float32)
    text_scores = lax.fori_loop(0, live_blocks, fill, empty)
    image_scores = (
        jnp.einsum("lrkgd,lrtkd->lrkgt", queries, image_keys, preferred_element_type=jnp.float32)
        * scale
    )
    local_top = jnp.maximum(jnp.max(text_scores, axis=-1), jnp.max(image_scores, axis=-1))
    text_weights = jnp.exp(text_scores - local_top[..., None])
    image_weights = jnp.exp(image_scores - local_top[..., None])
    local_total = jnp.sum(text_weights, axis=-1) + jnp.sum(image_weights, axis=-1)
    text_rounded = text_weights.astype(jnp.bfloat16)
    image_rounded = image_weights.astype(jnp.bfloat16)
    local_values = jnp.einsum(
        "lrkgt,lrtkd->lrkgd", image_rounded, image_values, preferred_element_type=jnp.float32
    )

    def add_values(index, carried):
        start = index * block
        weights_block = lax.dynamic_slice_in_dim(text_rounded, start, block, 4)
        values_block = lax.dynamic_slice_in_dim(text_values, start, block, 2)
        return carried + jnp.einsum(
            "lrkgt,lrtkd->lrkgd", weights_block, values_block, preferred_element_type=jnp.float32
        )

    local_values = lax.fori_loop(0, live_blocks, add_values, local_values)
    width_dev = query_width // seq_count
    merged = combined_all((local_top, local_total, local_values), "seq", merge_partials)
    result = (merged[2] / merged[1][..., None]).reshape(layers, req_dev, query_width)
    attended = lax.dynamic_slice_in_dim(result, seq_index * width_dev, width_dev, 2).astype(
        jnp.bfloat16
    )
    return (attended, image_cache)


def solution(mesh):
    return jax.shard_map(
        body,
        mesh=mesh,
        in_specs=(
            P(None, ("patch", "req"), None),
            P(None, ("patch", "req"), "seq", None),
            P(("patch", "req")),
            P(None, ("patch", "seq", "req"), None),
            P(("patch", "seq", "req")),
            P(("patch", "seq", "req")),
        ),
        out_specs=(P(None, ("patch", "req"), "seq"), P(None, ("patch", "req"), "seq", None)),
        check_vma=False,
    )
```

profile of v0, /device:TPU:6, one launch (start us, length us, event | category | flops | bytes accessed | tf_op | source)
XLA Modules:
  0.0 141.2 jit_solution(7268974834753334047)
XLA Ops:
  7.2 0.0 copy-start
  7.2 4.0 %sort.34 = (s32[256]{0:T(256)}, s32[256]{0:T(256)S(1)}) sort(s32[256]{0:T(256)} %param.14, s32[256]{0:T(256)S(1)} %iota.15), dimensions={0}, to_apply=%region_0.0 | sort | flops 2048 | bytes 4096 | tf_op jit(solution)/shard_map/jit(argsort)/sort | solution.py:74
  11.2 2.0 %gather_fusion.1 = s32[256]{0:T(256)S(1)} fusion(s32[256]{0:T(256)} %param.15, s32[1024]{0:T(1024)S(1)} %pad_clamp_fusion.1), kind=kCustom, calls=%fused_computation.1 | custom fusion | bytes 3072 | tf_op jit(solution)/shard_map/jit(_take)/gather | solution.py:76
  13.2 0.7 select_n.97
  13.9 12.1 %all-to-all-start.2 = ((s32[64,1,4]{2,1,0:T(1,128)}), s32[64,1,4]{2,1,0:T(1,128)S(1)}, u32[]{:S(2)}, u32[]{:S(2)}) async-start(s32[64,1,4]{2,1,0:T(1,128)} %bitcast.33), calls=%async_computation.2 | async-start | bytes 65536 | tf_op jit(solution)/shard_map/all_to_all | solution.py:80
  26.0 0.1 broadcast_in_dim.62
  26.1 0.0 copy-done
  26.1 8.2 %gather_fusion = bf16[256,4,1024]{2,0,1:T(8,128)(2,1)} fusion(bf16[4,256,1024]{2,1,0:T(8,128)(2,1)S(1)} %copy-done, s32[1024]{0:T(1024)S(1)} %pad_clamp_fusion.1), kind=kCustom, calls=%fused_computation | custom fusion | bytes 4195328 | tf_op jit(solution)/shard_map/jit(_take)/gather | solution.py:75
  34.3 3.2 %copy.52 = bf16[4,256,1024]{2,0,1:T(4,128)(2,1)S(1)} copy(bf16[4,256,1024]{2,1,0:T(8,128)(2,1)} %bitcast.95) | data formatting | bytes 4194304 | tf_op jit(solution)/shard_map/jit(_take)/gather | solution.py:75
  37.5 2.2 %broadcast_select_fusion = bf16[4,64,1,4,1024]{4,0,3,2,1:T(4,128)(2,1)} fusion(bf16[4,64,1,4,1024]{4,0,3,2,1:T(4,128)(2,1)S(1)} %bitcast.96, pred[64,4]{1,0:T(8,128)(4,1)S(1)} %broadcast_in_dim.62), kind=kLoop, calls=%fused_computation.20 | loop fusion | flops 1048576 | bytes 4194560 | tf_op jit(solution)/shard_map/jit(_take)/select_n | solution.py:75
  39.7 0.0 all-to-all-done.2
  39.7 10.6 %all-to-all-start = ((bf16[4,64,1,4,1024]{4,0,3,2,1:T(4,128)(2,1)}), bf16[4,64,1,4,1024]{4,0,3,2,1:T(4,128)(2,1)}, u32[]{:S(2)}, u32[]{:S(2)}) async-start(bf16[4,64,1,4,1024]{4,0,3,2,1:T(4,128)(2,1)} %broadcast_select_fusion), calls=%async_computation | async-start | bytes 4194304 | tf_op jit(solution)/shard_map/all_to_all | solution.py:78
  50.2 0.0 sort.37.cloned.1.call-start
  50.9 5.9 %fusion.31 = (bf16[4,1,768,512]{3,2,1,0:T(8,128)(2,1)}, bf16[4,1,768,512]{3,2,1,0:T(8,128)(2,1)}) fusion(bf16[4,1,768,1024]{3,2,1,0:T(8,128)(2,1)} %param.11), kind=kLoop, calls=%fused_computation.67 | loop fusion | bytes 12582912 | tf_op jit(solution)/shard_map/slice | solution.py:89
  56.8 0.0 copy-start.2
  56.8 4.7 %copy.55 = bf16[4,1,768,512]{2,3,0,1:T(8,128)(2,1)} copy(bf16[4,1,768,512]{3,2,1,0:T(8,128)(2,1)} %get-tuple-element.135) | data formatting | bytes 6291456
  61.5 0.0 copy-done.2
  61.6 0.1 subtract_reduce_fusion
  61.7 0.7 sub.76
  62.4 0.6 iota.17
  63.0 0.0 sort.37.cloned.1.call-update
  63.1 0.6 reshape.307
  63.7 0.1 reduce_max.16
  63.8 4.7 %copy.56 = bf16[4,1,768,512]{2,3,0,1:T(8,128)(2,1)} copy(bf16[4,1,768,512]{3,2,1,0:T(8,128)(2,1)} %get-tuple-element.134) | data formatting | bytes 6291456
  68.5 0.0 sort.37.cloned.1.call-done
  68.5 0.7 compare_select_fusion
  69.2 0.6 pad_clamp_fusion
  69.8 1.2 compare_and_fusion
  71.0 30.4 %all-to-all-done = bf16[4,64,1,4,1024]{4,0,3,2,1:T(4,128)(2,1)} async-done(((bf16[4,64,1,4,1024]{4,0,3,2,1:T(4,128)(2,1)}), bf16[4,64,1,4,1024]{4,0,3,2,1:T(4,128)(2,1)}, u32[]{:S(2)}, u32[]{:S(2)}) %all-to-all-start) | async-done | bytes 2097184 | tf_op jit(solution)/shard_map/all_to_all | solution.py:78
  101.4 3.6 %fusion.32 = (bf16[4,1,256,512]{3,0,2,1:T(4,128)(2,1)}, bf16[4,1,256,512]{3,0,2,1:T(4,128)(2,1)}) fusion(bf16[4,1,256,1024]{3,0,2,1:T(4,128)(2,1)} %bitcast.9), kind=kLoop, calls=%fused_computation.68 | loop fusion | bytes 4194304 | tf_op jit(solution)/shard_map/slice | solution.py:91
  105.0 1.6 %copy.33 = bf16[4,1,256,512]{2,3,0,1:T(8,128)(2,1)S(1)} copy(bf16[4,1,256,512]{3,0,2,1:T(4,128)(2,1)} %get-tuple-element.137) | data formatting | bytes 2097152 | tf_op jit(solution)/shard_map/slice | solution.py:90
  106.6 1.6 %fusion.34 = (f32[4,4,7]{2,1,0:T(4,128)S(1)}, f32[4,4,7,256]{3,2,1,0:T(8,128)}) fusion(bf16[4,256,4,128]{1,3,2,0:T(8,128)(2,1)S(1)} %bitcast.98, bf16[4,4,7,128]{3,2,1,0:T(8,128)(2,1)} %reshape.307), kind=kOutput, calls=%fused_computation.70 | convolution fusion | flops 7397264 | bytes 1192384 | tf_op jit(solution)/shard_map/lrkgd,lrtkd->lrkgt/dot_general | solution.py:116
  108.3 0.8 fusion.15
  109.1 0.0 copy-start.1
  109.1 0.1 max.27
  109.2 1.6 %copy.37 = bf16[4,1,256,512]{2,3,0,1:T(8,128)(2,1)S(1)} copy(bf16[4,1,256,512]{3,0,2,1:T(4,128)(2,1)} %get-tuple-element.136) | data formatting | bytes 2097152 | tf_op jit(solution)/shard_map/slice | solution.py:91
  110.8 0.0 copy-done.1
  110.8 0.2 fusion.16
  111.0 0.4 convolution_bitcast_fusion.1
  111.5 0.1 add.107
  111.6 0.7 broadcast_in_dim.67
  112.3 8.8 %all-to-all-start.1 = ((f32[4,114,128]{2,1,0:T(8,128)}), f32[4,114,128]{2,1,0:T(8,128)S(1)}, u32[]{:S(2)}, u32[]{:S(2)}) async-start(f32[4,114,128]{2,1,0:T(8,128)} %broadcast_in_dim.67), calls=%async_computation.1 | async-start | bytes 491520 | tf_op jit(solution)/shard_map/all_to_all | solution.py:15
  121.1 0.0 copy-start.3
  121.1 5.4 %gather_fusion.2 = bf16[256,4,1024]{2,1,0:T(4,128)(2,1)} fusion(bf16[4,256,1024]{2,0,1:T(4,128)(2,1)} %bitcast.35, s32[1024]{0:T(1024)} %pad_clamp_fusion), kind=kCustom, calls=%fused_computation.2 | custom fusion | bytes 4195328 | tf_op jit(solution)/shard_map/jit(take_along_axis)/gather | solution.py:86
  126.5 0.0 copy-done.3
  126.5 2.7 %bitcast_select_fusion = bf16[4,1,256,1024]{3,0,2,1:T(4,128)(2,1)S(1)} fusion(bf16[256,4,1024]{2,1,0:T(4,128)(2,1)} %gather_fusion.2, pred[256]{0:T(512)(128)(4,1)S(1)} %copy-done.3), kind=kLoop, calls=%fused_computation.19 | loop fusion | flops 1048576 | bytes 4194560 | tf_op jit(solution)/shard_map/jit(take_along_axis)/select_n | solution.py:86
  129.2 1.9 %copy.49 = bf16[4,1,256,1024]{3,2,1,0:T(8,128)(2,1)} copy(bf16[4,1,256,1024]{3,0,2,1:T(4,128)(2,1)S(1)} %bitcast_select_fusion) | data formatting | bytes 4194304
  131.1 0.0 all-to-all-done.1
  131.1 0.1 copy.44
  131.2 0.5 slice.80
  131.8 0.5 slice.81
  132.3 0.1 reshape.316
  132.4 0.1 reshape.318
  132.6 0.2 copy.45
  132.8 0.2 copy.43
  133.0 0.3 multiply_add_fusion
  133.3 0.3 fusion.21
  133.6 0.1 div.33
  133.8 0.6 fusion.22
  (21 shorter events, 0.3 us)
Async XLA Ops:
  7.2 19.0 %copy-start = (bf16[4,256,1024]{2,1,0:T(8,128)(2,1)S(1)}, bf16[4,256,1024]{2,1,0:T(8,128)(2,1)}, u32[]{:S(2)}) copy-start(bf16[4,256,1024]{2,1,0:T(8,128)(2,1)} %param.13) | copy-start | bytes 6291460
  13.9 25.8 %all-to-all-start.2 = ((s32[64,1,4]{2,1,0:T(1,128)}), s32[64,1,4]{2,1,0:T(1,128)S(1)}, u32[]{:S(2)}, u32[]{:S(2)}) async-start(s32[64,1,4]{2,1,0:T(1,128)} %bitcast.33), calls=%async_computation.2 | async-start | bytes 65536 | tf_op jit(solution)/shard_map/all_to_all | solution.py:80
  39.7 61.7 %all-to-all-start = ((bf16[4,64,1,4,1024]{4,0,3,2,1:T(4,128)(2,1)}), bf16[4,64,1,4,1024]{4,0,3,2,1:T(4,128)(2,1)}, u32[]{:S(2)}, u32[]{:S(2)}) async-start(bf16[4,64,1,4,1024]{4,0,3,2,1:T(4,128)(2,1)} %broadcast_select_fusion), calls=%async_computation | async-start | bytes 4194304 | tf_op jit(solution)/shard_map/all_to_all | solution.py:78
  50.2 18.3 %sort.37.cloned.1.call-start = ((), (), s32[]{:S(2)}) async-start(), calls=%async_computation.3 | async-start | bytes 6176 | tf_op jit(solution)/shard_map/jit(argsort)/sort | solution.py:85
  56.8 4.7 %copy-start.2 = (bf16[4,1,3584]{2,0,1:T(4,128)(2,1)S(1)}, bf16[4,1,3584]{2,0,1:T(4,128)(2,1)}, u32[]{:S(2)}) copy-start(bf16[4,1,3584]{2,0,1:T(4,128)(2,1)} %param.10) | copy-start | bytes 86020
  109.1 1.7 %copy-start.1 = (f32[4,4,7,256]{3,2,1,0:T(8,128)S(1)}, f32[4,4,7,256]{3,2,1,0:T(8,128)}, u32[]{:S(2)}) copy-start(f32[4,4,7,256]{3,2,1,0:T(8,128)} %get-tuple-element.148) | copy-start | bytes 344068
  112.3 18.8 %all-to-all-start.1 = ((f32[4,114,128]{2,1,0:T(8,128)}), f32[4,114,128]{2,1,0:T(8,128)S(1)}, u32[]{:S(2)}, u32[]{:S(2)}) async-start(f32[4,114,128]{2,1,0:T(8,128)} %broadcast_in_dim.67), calls=%async_computation.1 | async-start | bytes 491520 | tf_op jit(solution)/shard_map/all_to_all | solution.py:15
  121.1 5.4 %copy-start.3 = (pred[256]{0:T(512)(128)(4,1)S(1)}, pred[256]{0:T(512)(128)(4,1)}, u32[]{:S(2)}) copy-start(pred[256]{0:T(512)(128)(4,1)} %compare_and_fusion) | copy-start | bytes 772
Sparse Core Ops, SparseCore 0:
  63.1 2.5 sort.39.cloned.1.call-done
  (1 shorter events, 0.0 us)
where the time goes:
time: 143 us; the launch traced here: 141 us
  local copies, waits for them, and re-layouts  48.5 us (34%)
  starting transfers between devices  31.5 us (22%)
  waiting for transfers between devices  30.4 us (21%)
  between operations  15 us (10%)
  other arithmetic  13.8 us (10%)
  matrix products  2.06 us (1%)
    all_to_all x1, waiting for transfers between devices, body(): lax.all_to_all(sending, ('patch', 'req'), split_axis=1, concat_axis=3, ti...  30.4 us
    all_to_all x1, starting transfers between devices, body(): lax.all_to_all(place_send, ('patch', 'req'), split_axis=0, concat_axis=2,...  12.1 us
    unnamed x12, local copies, waits for them, and re-layouts  11.4 us
    gather x2, local copies, waits for them, and re-layouts, body(): grouped = jnp.take(image_rows, order, axis=1)  11.4 us
    all_to_all x1, starting transfers between devices, body(): lax.all_to_all(sending, ('patch', 'req'), split_axis=1, concat_axis=3, ti...  10.6 us
    all_to_all x1, starting transfers between devices, copy_for_each(): return lax.all_to_all(copies, axis, split_axis=0, concat_axis=0, tiled=True)  8.8 us
    slice x1, local copies, waits for them, and re-layouts, body(): text_cache[..., kv_width:]  5.9 us
    gather x1, local copies, waits for them, and re-layouts, body(): jnp.take_along_axis(image_block, inverse[None, :, :, None], axis=2)  5.37 us
  transfers between devices with their start and end apart: 3, of which 1 were waited for; matrix products, arithmetic and copies ran while one was open for 31% of the time, Pallas kernels for 0%

commit v1 on v0

v1 whole, which is shorter than its diff:
```python
import functools
import math

import jax
import jax.numpy as jnp
from jax import lax
from jax.experimental import pallas as pl
from jax.experimental.pallas import tpu as pltpu
from jax.sharding import PartitionSpec as P

HEADS = 28
KV_HEADS = 4
HEAD_DIM = 128
GROUP = HEADS // KV_HEADS
PAD = 8
MESH = pl.DeviceIdType.MESH
BF16 = jnp.bfloat16
F32 = jnp.float32
CHUNKS = ((0, 512), (512, 256), (768, 256))


def kernel(
    dims,
    pm_hbm, pos_hbm, len_ref, query_hbm, text_hbm, rows_hbm,
    att_ref, cache_ref,
    pm_ref, pos_ref, query_ref, text_ref, rows_ref,
    sort_ref, send_ref, got_ref, place_ref,
    place_send, place_got, q_ref, score_ref, weight_ref, acc_ref, stat_ref, acc_got, stat_got,
    in_sems, send_sem, recv_sems, place_sem, xsend_sem, xstat_sem, xacc_sem,
):
    patches, seqs, reqs, layers, slot, band, text_dev = dims
    peers = patches * reqs
    msg = layers * slot
    total_rows = layers * band
    patch, seq, req = (lax.axis_index(n) for n in ("patch", "seq", "req"))
    me = patch * reqs + req
    scale = 1.0 / math.sqrt(HEAD_DIM)
    n_chunks = len(CHUNKS)

    def peer(step):
        other = lax.rem(me + step, peers)
        return other, {"patch": other // reqs, "req": lax.rem(other, reqs)}

    loads = [
        pltpu.make_async_copy(src, dst, in_sems.at[i])
        for i, (src, dst) in enumerate(
            (
                (pm_hbm, pm_ref),
                (pos_hbm, pos_ref),
                (rows_hbm, rows_ref),
                (query_hbm, query_ref),
                (text_hbm, text_ref),
            )
        )
    ]
    loads[0].start()
    loads[1].start()
    loads[2].start()

    barrier = pltpu.get_barrier_semaphore()

    def greet(step, carry):
        _, device = peer(step)
        pl.semaphore_signal(barrier, inc=1, device_id=device, device_id_type=MESH)
        return carry

    lax.fori_loop(1, peers, greet, 0)
    for step in range(1, seqs):
        pl.semaphore_signal(
            barrier, inc=1, device_id={"seq": lax.rem(seq + step, seqs)}, device_id_type=MESH
        )
    loads[3].start()
    loads[4].start()

    loads[0].wait()
    loads[1].wait()
    owner = pm_ref[...]
    member = lax.broadcasted_iota(jnp.int32, (peers, band), 0) == owner
    member_f = member.astype(F32)
    before = lax.broadcasted_iota(jnp.int32, (band, band), 0) < lax.broadcasted_iota(
        jnp.int32, (band, band), 1
    )
    counts = jnp.dot(
        member_f.astype(BF16), before.astype(F32).astype(BF16), preferred_element_type=F32
    )
    rank = jnp.sum(member_f * counts, axis=0, keepdims=True)
    target = owner.astype(F32) * msg + rank
    line = lax.broadcasted_iota(jnp.int32, (total_rows, band), 0).astype(F32)
    for l in range(layers):
        sort_ref[:, l * band : (l + 1) * band] = (
            (line == target + float(l * slot)).astype(F32).astype(BF16)
        )

    local = pos_ref[...].astype(F32) - (seq * band).astype(F32)
    lane = lax.broadcasted_iota(jnp.int32, (peers, 128), 1)
    spread = ((lane // slot) % layers * band).astype(F32)
    for k in range(slot):
        mine = jnp.where(member & (counts == float(k)), local, 0.0)
        spread = spread + jnp.where(lane % slot == k, jnp.sum(mine, axis=1, keepdims=True), 0.0)
    place_send[...] = spread.reshape(peers, 1, 128)

    loads[2].wait()

    def sort_chunk(c):
        start, width = CHUNKS[c]
        for j in range(start, start + width, 256):
            def rows_of(i, carry):
                lines = pl.ds(pl.multiple_of(i * 256, 256), 256)
                send_ref[lines, j : j + 256] = jnp.dot(
                    sort_ref[lines, :], rows_ref[:, j : j + 256], preferred_element_type=F32
                ).astype(BF16)
                return carry
            lax.fori_loop(0, total_rows // 256, rows_of, 0)

    def block(ref, index, c):
        start, width = CHUNKS[c]
        return ref.at[pl.ds(pl.multiple_of(index * msg, msg), msg), pl.ds(start, width)]

    def send_chunk(c):
        def send(step, carry):
            other, device = peer(step)
            pltpu.make_async_remote_copy(
                src_ref=block(send_ref, other, c),
                dst_ref=block(got_ref, me, c),
                send_sem=send_sem,
                recv_sem=recv_sems.at[c],
                device_id=device,
                device_id_type=MESH,
            ).start()
            return carry
        lax.fori_loop(1, peers, send, 0)

    sort_chunk(0)
    pl.semaphore_wait(barrier, peers - 1 + seqs - 1)

    def send_place(step, carry):
        other, device = peer(step)
        pltpu.make_async_remote_copy(
            src_ref=place_send.at[other],
            dst_ref=place_got.at[me],
            send_sem=send_sem,
            recv_sem=place_sem,
            device_id=device,
            device_id_type=MESH,
        ).start()
        return carry

    lax.fori_loop(1, peers, send_place, 0)
    send_chunk(0)
    for c in range(1, n_chunks):
        sort_chunk(c)
        send_chunk(c)
    own = pl.ds(pl.multiple_of(me * msg, msg), msg)
    got_ref[own, :] = send_ref[own, :]
    place_got[pl.ds(me, 1)] = place_send[pl.ds(me, 1)]

    loads[3].wait()
    q_ref[...] = jnp.zeros_like(q_ref)
    for l in range(layers):
        whole = query_ref[l].astype(F32)
        for h in range(HEADS):
            g, k = divmod(h, GROUP)
            q_ref[g, l * PAD + k : l * PAD + k + 1, :] = whole[:, h * HEAD_DIM : (h + 1) * HEAD_DIM]

    loads[4].wait()
    length = len_ref[0]
    text_at = lax.broadcasted_iota(jnp.int32, (PAD, text_dev), 1) + seq * text_dev
    used = text_at < length

    def dot_t(a, b):
        return lax.dot_general(a, b, (((1,), (1,)), ((), ())), preferred_element_type=F32)

    for g in range(KV_HEADS):
        keys = slice(g * HEAD_DIM, (g + 1) * HEAD_DIM)
        for l in range(layers):
            lines = slice(l * PAD, (l + 1) * PAD)
            raw = dot_t(q_ref[g, lines, :].astype(BF16), text_ref[l, :, keys]) * scale
            score_ref[g, lines, :] = jnp.where(used, raw, -jnp.inf)

    def wait_all(sem, ref):
        pltpu.make_async_copy(ref, ref, sem).wait()

    wait_all(place_sem, place_got.at[pl.ds(0, peers - 1)])
    per_tile = 128 // msg
    first = lax.broadcasted_iota(jnp.int32, (per_tile, 128), 0)
    which = lax.broadcasted_iota(jnp.int32, (per_tile, 128), 1) // msg
    cache_line = lax.broadcasted_iota(jnp.int32, (total_rows, 128), 0).astype(F32)
    for b in range(peers // per_tile):
        tile = place_got[b * per_tile : (b + 1) * per_tile].reshape(per_tile, 128)
        to = jnp.sum(jnp.where(first == which, tile, 0.0), axis=0, keepdims=True)
        place_ref[:, b * 128 : (b + 1) * 128] = (cache_line == to).astype(F32).astype(BF16)

    def place_chunk(c):
        start, width = CHUNKS[c]
        for j in range(start, start + width, 256):
            def rows_of(i, carry):
                lines = pl.ds(pl.multiple_of(i * 256, 256), 256)
                cache_ref[lines, j : j + 256] = jnp.dot(
                    place_ref[lines, :], got_ref[:, j : j + 256], preferred_element_type=F32
                ).astype(BF16)
                return carry
            lax.fori_loop(0, total_rows // 256, rows_of, 0)

    def wait_chunk(c):
        start, width = CHUNKS[c]
        wait_all(
            recv_sems.at[c], got_ref.at[pl.ds(0, (peers - 1) * msg), pl.ds(start, width)]
        )

    def exchange(src_ref, dst_ref, g, sem):
        @pl.when(seq != g)
        def _():
            pltpu.make_async_remote_copy(
                src_ref=src_ref.at[g],
                dst_ref=dst_ref.at[seq],
                send_sem=xsend_sem,
                recv_sem=sem,
                device_id={"seq": g},
                device_id_type=MESH,
            ).start()

    wait_chunk(0)
    same_layer = (
        lax.broadcasted_iota(jnp.int32, (layers * PAD, total_rows), 1) // slot
    ) % layers == lax.broadcasted_iota(jnp.int32, (layers * PAD, total_rows), 0) // PAD
    half = lax.broadcasted_iota(jnp.int32, (layers * PAD, 128), 1) < 64
    for g in range(KV_HEADS):
        keys = slice(g * HEAD_DIM, (g + 1) * HEAD_DIM)
        vals = slice((KV_HEADS + g) * HEAD_DIM, (KV_HEADS + g + 1) * HEAD_DIM)
        raw = dot_t(q_ref[g].astype(BF16), got_ref[:, keys]) * scale
        image = jnp.where(same_layer, raw, -jnp.inf)
        text = score_ref[g]
        top = jnp.maximum(
            jnp.max(image, axis=1, keepdims=True), jnp.max(text, axis=1, keepdims=True)
        )
        image_w = jnp.exp(image - top)
        text_w = jnp.exp(text - top)
        total = jnp.sum(image_w, axis=1, keepdims=True) + jnp.sum(text_w, axis=1, keepdims=True)
        weight_ref[g] = image_w.astype(BF16)
        stat_ref[g] = jnp.where(half, top, total)
        for l in range(layers):
            lines = slice(l * PAD, (l + 1) * PAD)
            acc_ref[g, lines, :] = jnp.dot(
                text_w[lines].astype(BF16), text_ref[l, :, vals], preferred_element_type=F32
            )
    for g in range(KV_HEADS):
        exchange(stat_ref, stat_got, g, xstat_sem)
    stat_got[pl.ds(seq, 1)] = stat_ref[pl.ds(seq, 1)]
    place_chunk(0)

    for c in range(1, n_chunks):
        wait_chunk(c)
        start, width = CHUNKS[c]
        heads = range(start // HEAD_DIM - KV_HEADS, (start + width) // HEAD_DIM - KV_HEADS)
        for g in heads:
            vals = slice((KV_HEADS + g) * HEAD_DIM, (KV_HEADS + g + 1) * HEAD_DIM)
            acc_ref[g] = acc_ref[g] + jnp.dot(
                weight_ref[g], got_ref[:, vals], preferred_element_type=F32
            )
        for g in heads:
            exchange(acc_ref, acc_got, g, xacc_sem)
        place_chunk(c)
    acc_got[pl.ds(seq, 1)] = acc_ref[pl.ds(seq, 1)]

    wait_all(xstat_sem, stat_got.at[pl.ds(0, seqs - 1)])
    tops = [stat_got[b][:, 0:1] for b in range(seqs)]
    totals = [stat_got[b][:, 64:65] for b in range(seqs)]
    top = functools.reduce(jnp.maximum, tops)
    factors = [jnp.exp(t - top) for t in tops]
    total = sum(f * t for f, t in zip(factors, totals))
    wait_all(xacc_sem, acc_got.at[pl.ds(0, seqs - 1)])
    summed = sum(f * acc_got[b] for b, f in enumerate(factors))
    result = summed / total
    for l in range(layers):
        for k in range(GROUP):
            att_ref[l, :, k * HEAD_DIM : (k + 1) * HEAD_DIM] = result[
                l * PAD + k : l * PAD + k + 1, :
            ].astype(BF16)

    for c in range(n_chunks):
        start, width = CHUNKS[c]
        wait_all(send_sem, got_ref.at[pl.ds(0, (peers - 1) * msg), pl.ds(start, width)])
    wait_all(send_sem, place_got.at[pl.ds(0, peers - 1)])
    wait_all(xsend_sem, stat_got.at[pl.ds(0, seqs - 1)])
    wait_all(xsend_sem, acc_got.at[pl.ds(0, seqs - 1)])


def body(query, text_cache, text_len, image_rows, patch_map, image_places):
    layers = query.shape[0]
    text_dev = text_cache.shape[2]
    width = text_cache.shape[3]
    band = image_rows.shape[1]
    patches, seqs, reqs = (lax.axis_size(n) for n in ("patch", "seq", "req"))
    peers = patches * reqs
    slot = band // peers
    rows = layers * band
    heads = layers * PAD
    dims = (patches, seqs, reqs, layers, slot, band, text_dev)
    hbm = pl.BlockSpec(memory_space=pl.ANY)
    vmem = pl.BlockSpec(memory_space=pltpu.VMEM)
    attended, cache = pl.pallas_call(
        functools.partial(kernel, dims),
        name="reshard_attend",
        out_shape=(
            jax.ShapeDtypeStruct((layers, 1, GROUP * HEAD_DIM), BF16),
            jax.ShapeDtypeStruct((rows, width), BF16),
        ),
        in_specs=[hbm, hbm, pl.BlockSpec(memory_space=pltpu.SMEM), hbm, hbm, hbm],
        out_specs=(vmem, vmem),
        scratch_shapes=[
            pltpu.VMEM((1, band), jnp.int32),
            pltpu.VMEM((1, band), jnp.int32),
            pltpu.VMEM(query.shape, BF16),
            pltpu.VMEM((layers, text_dev, width), BF16),
            pltpu.VMEM((rows, width), BF16),
            pltpu.VMEM((rows, rows), BF16),
            pltpu.VMEM((rows, width), BF16),
            pltpu.VMEM((rows, width), BF16),
            pltpu.VMEM((rows, rows), BF16),
            pltpu.VMEM((peers, 1, 128), F32),
            pltpu.VMEM((peers, 1, 128), F32),
            pltpu.VMEM((KV_HEADS, heads, HEAD_DIM), F32),
            pltpu.VMEM((KV_HEADS, heads, text_dev), F32),
            pltpu.VMEM((KV_HEADS, heads, rows), BF16),
            pltpu.VMEM((KV_HEADS, heads, HEAD_DIM), F32),
            pltpu.VMEM((KV_HEADS, heads, HEAD_DIM), F32),
            pltpu.VMEM((seqs, heads, HEAD_DIM), F32),
            pltpu.VMEM((seqs, heads, HEAD_DIM), F32),
            pltpu.SemaphoreType.DMA((5,)),
            pltpu.SemaphoreType.DMA,
            pltpu.SemaphoreType.DMA((len(CHUNKS),)),
            pltpu.SemaphoreType.DMA,
            pltpu.SemaphoreType.DMA,
            pltpu.SemaphoreType.DMA,
            pltpu.SemaphoreType.DMA,
        ],
        compiler_params=pltpu.CompilerParams(
            collective_id=0, has_side_effects=True, vmem_limit_bytes=48 * 1024 * 1024
        ),
    )(
        patch_map.reshape(1, band),
        image_places.reshape(1, band),
        text_len,
        query,
        text_cache.reshape(layers, text_dev, width),
        image_rows.reshape(rows, width),
    )
    return attended, cache.reshape(layers, 1, band, width)


def solution(mesh):
    return jax.shard_map(
        body,
        mesh=mesh,
        in_specs=(
            P(None, ("patch", "req"), None),
            P(None, ("patch", "req"), "seq", None),
            P(("patch", "req")),
            P(None, ("patch", "seq", "req"), None),
            P(("patch", "seq", "req")),
            P(("patch", "seq", "req")),
        ),
        out_specs=(P(None, ("patch", "req"), "seq"), P(None, ("patch", "req"), "seq", None)),
        check_vma=False,
    )
```

time: 143 us -> 70.2 us (0.49); the launches traced: 141 us -> 70 us
  Pallas kernels: 0 us -> 63 us
  local copies, waits for them, and re-layouts: 48.5 us -> 5.65 us
  starting transfers between devices: 31.5 us -> 0 us
  waiting for transfers between devices: 30.4 us -> 0 us
  other arithmetic: 13.8 us -> 0 us
  between operations: 15 us -> 1.3 us
  matrix products: 2.06 us -> 0 us
    pallas_call x0 -> x1, Pallas kernels: none -> 63 us  [body(): pl.pallas_call(functools.partial(kernel, dims), name='reshard_attend', ou...]
    all_to_all x3 -> x0, starting transfers between devices: 31.5 us -> none  [the longest x1 12.1 us: body(): lax.all_to_all(place_send, ('patch', 'req'), split_axis=0, concat_axis=2,...]
    all_to_all x3 -> x0, waiting for transfers between devices: 30.4 us -> none  [the longest x1 30.4 us: body(): lax.all_to_all(sending, ('patch', 'req'), split_axis=1, concat_axis=3, ti...]
    gather x4 -> x0, local copies, waits for them, and re-layouts: 18.7 us -> none  [the longest x2 11.4 us: body(): grouped = jnp.take(image_rows, order, axis=1)]
    slice x9 -> x0, local copies, waits for them, and re-layouts: 13.9 us -> none  [the longest x1 5.9 us: body(): text_cache[..., kv_width:]]
    unnamed x12 -> x9, local copies, waits for them, and re-layouts: 11.4 us -> 5.65 us
    select_n x5 -> x0, other arithmetic: 5.51 us -> none  [the longest x2 3.35 us: body(): jnp.take_along_axis(image_block, inverse[None, :, :, None], axis=2)]
    sort x1 -> x0, other arithmetic: 3.99 us -> none  [body(): order = jnp.argsort(patch_map, stable=True)]
  transfers between devices with their start and end apart: 3 -> 0, of which waited for: 1 -> 0; matrix products, arithmetic and copies ran while one was open for 31% -> 0% of each run, Pallas kernels for 0% -> 0%
where the time goes in v1:
time: 70.2 us; the launch traced here: 70 us
  Pallas kernels  63 us (90%)
  local copies, waits for them, and re-layouts  5.65 us (8%)
  between operations  1.3 us (2%)
    pallas_call x1, Pallas kernels, body(): pl.pallas_call(functools.partial(kernel, dims), name='reshard_attend', ou...  63 us
    unnamed x9, local copies, waits for them, and re-layouts  5.65 us

profile of v1, /device:TPU:6, one launch (start us, length us, event | category | flops | bytes accessed | tf_op | source)
XLA Modules:
  0.0 70.0 jit_solution(1611001741655923609)
XLA Ops:
  1.3 0.8 %copy.8.query_hbm = bf16[4,1,3584]{2,1,0:T(2,128)(2,1)S(1)} copy(bf16[4,1,3584]{2,0,1:T(4,128)(2,1)} %param.6) | data formatting | bytes 57344 | tf_op args[0]
  2.1 0.0 copy-start
  2.1 1.6 %copy-done = bf16[4,256,1024]{2,1,0:T(8,128)(2,1)S(1)} copy-done((bf16[4,256,1024]{2,1,0:T(8,128)(2,1)S(1)}, bf16[4,256,1024]{2,1,0:T(8,128)(2,1)}, u32[]{:S(2)}) %copy-start) | copy-done | bytes 2097176
  3.7 0.0 copy-start.1
  3.7 0.7 copy-done.1
  4.3 0.0 copy-start.2
  4.3 0.7 copy-done.2
  5.0 63.0 %reshard_attend.1 = (bf16[4,1,896]{2,1,0:T(2,128)(2,1)S(1)}, bf16[1024,1024]{1,0:T(8,128)(2,1)S(1)}) custom-call(s32[1,256]{1,0:T(1,128)S(1)} %bitcast.9, s32[1,256]{1,0:T(1,128)S(1)} %bitcast.10, s32[1]{0:T(128)S(6)} %copy.12.len_ref, bf16[4,1,3584]{2,1,0:T(2,128)(2,1)S(1)} %copy.8.query_hbm, bf16[4,768,1024]{2,1,0:T(8,128)(2,1)} %bitcast.11, ...), custom_call_target="tpu_custom_call" | custom-call | tf_op jit(solution)/shard_map/reshard_attend/pallas_call | solution.py:301
  68.1 0.6 copy.9
  68.7 1.3 %copy.13 = bf16[4,1,256,1024]{3,2,1,0:T(8,128)(2,1)} copy(bf16[4,1,256,1024]{3,2,1,0:T(8,128)(2,1)S(1)} %bitcast.7) | data formatting | bytes 4194304
Async XLA Ops:
  2.1 1.6 %copy-start = (bf16[4,256,1024]{2,1,0:T(8,128)(2,1)S(1)}, bf16[4,256,1024]{2,1,0:T(8,128)(2,1)}, u32[]{:S(2)}) copy-start(bf16[4,256,1024]{2,1,0:T(8,128)(2,1)} %param.9) | copy-start | bytes 6291460
  3.7 0.7 copy-start.1
  4.3 0.7 copy-start.2

commit v2 on v1

--- a/solution.py
+++ b/solution.py
@@ -21,7 +21,7 @@
 
 def kernel(
     dims,
-    pm_hbm, pos_hbm, len_ref, query_hbm, text_hbm, rows_hbm,
+    len_ref, pm_hbm, pos_hbm, query_hbm, text_hbm, rows_hbm,
     att_ref, cache_ref,
     pm_ref, pos_ref, query_ref, text_ref, rows_ref,
     sort_ref, send_ref, got_ref, place_ref,
@@ -157,7 +157,7 @@
     loads[3].wait()
     q_ref[...] = jnp.zeros_like(q_ref)
     for l in range(layers):
-        whole = query_ref[l].astype(F32)
+        whole = query_ref[l : l + 1, :].astype(F32)
         for h in range(HEADS):
             g, k = divmod(h, GROUP)
             q_ref[g, l * PAD + k : l * PAD + k + 1, :] = whole[:, h * HEAD_DIM : (h + 1) * HEAD_DIM]
@@ -273,7 +273,7 @@
     result = summed / total
     for l in range(layers):
         for k in range(GROUP):
-            att_ref[l, :, k * HEAD_DIM : (k + 1) * HEAD_DIM] = result[
+            att_ref[l : l + 1, k * HEAD_DIM : (k + 1) * HEAD_DIM] = result[
                 l * PAD + k : l * PAD + k + 1, :
             ].astype(BF16)
 
@@ -296,21 +296,21 @@
     rows = layers * band
     heads = layers * PAD
     dims = (patches, seqs, reqs, layers, slot, band, text_dev)
-    hbm = pl.BlockSpec(memory_space=pl.ANY)
+    hbm = pl.BlockSpec(memory_space=pltpu.HBM)
     vmem = pl.BlockSpec(memory_space=pltpu.VMEM)
     attended, cache = pl.pallas_call(
         functools.partial(kernel, dims),
         name="reshard_attend",
         out_shape=(
-            jax.ShapeDtypeStruct((layers, 1, GROUP * HEAD_DIM), BF16),
+            jax.ShapeDtypeStruct((layers, GROUP * HEAD_DIM), BF16),
             jax.ShapeDtypeStruct((rows, width), BF16),
         ),
-        in_specs=[hbm, hbm, pl.BlockSpec(memory_space=pltpu.SMEM), hbm, hbm, hbm],
+        in_specs=[pl.BlockSpec(memory_space=pltpu.SMEM)] + [hbm] * 5,
         out_specs=(vmem, vmem),
         scratch_shapes=[
             pltpu.VMEM((1, band), jnp.int32),
             pltpu.VMEM((1, band), jnp.int32),
-            pltpu.VMEM(query.shape, BF16),
+            pltpu.VMEM((layers, HEADS * HEAD_DIM), BF16),
             pltpu.VMEM((layers, text_dev, width), BF16),
             pltpu.VMEM((rows, width), BF16),
             pltpu.VMEM((rows, rows), BF16),
@@ -338,14 +338,19 @@
             collective_id=0, has_side_effects=True, vmem_limit_bytes=48 * 1024 * 1024
         ),
     )(
-        patch_map.reshape(1, band),
-        image_places.reshape(1, band),
         text_len,
-        query,
-        text_cache.reshape(layers, text_dev, width),
-        image_rows.reshape(rows, width),
+        *(
+            pltpu.with_memory_space_constraint(x, pltpu.HBM)
+            for x in (
+                patch_map.reshape(1, band),
+                image_places.reshape(1, band),
+                query.reshape(layers, HEADS * HEAD_DIM),
+                text_cache.reshape(layers, text_dev, width),
+                image_rows.reshape(rows, width),
+            )
+        ),
     )
-    return attended, cache.reshape(layers, 1, band, width)
+    return attended.reshape(layers, 1, GROUP * HEAD_DIM), cache.reshape(layers, 1, band, width)
 
 
 def solution(mesh):

time: 70.2 us -> 66.1 us (0.942)
  local copies, waits for them, and re-layouts: 5.65 us -> 1.91 us
    unnamed x9 -> x2, local copies, waits for them, and re-layouts: 5.65 us -> 1.91 us
where the time goes in v2:
time: 66.1 us
  Pallas kernels  62.9 us (95%)
  local copies, waits for them, and re-layouts  1.91 us (3%)
  between operations  1.28 us (2%)
    pallas_call x1, Pallas kernels, body(): pl.pallas_call(functools.partial(kernel, dims), name='reshard_attend', ou...  62.9 us
    unnamed x2, local copies, waits for them, and re-layouts  1.91 us

profile of v2, /device:TPU:6, one launch (start us, length us, event | category | flops | bytes accessed | tf_op | source)
XLA Modules:
  0.0 66.1 jit_solution(10005593685195996965)
XLA Ops:
  1.3 62.9 %reshard_attend.1 = (bf16[4,896]{1,0:T(4,128)(2,1)S(1)}, bf16[1024,1024]{1,0:T(8,128)(2,1)S(1)}) custom-call(s32[1]{0:T(128)S(6)} %copy.11.len_ref, s32[1,256]{1,0:T(1,128)} %bitcast.14, s32[1,256]{1,0:T(1,128)} %bitcast.15, bf16[4,3584]{1,0:T(4,128)(2,1)} %bitcast.13, bf16[4,768,1024]{2,1,0:T(8,128)(2,1)} %bitcast.11, bf16[1024,1024]{1,0:T(8,128)(2,1)} %bitcast.12), custom_call_target="tpu_custom_call" | custom-call | tf_op jit(solution)/shard_map/reshard_attend/pallas_call | solution.py:301
  64.1 0.6 copy.12
  64.7 1.3 %copy.13 = bf16[4,1,256,1024]{3,2,1,0:T(8,128)(2,1)} copy(bf16[4,1,256,1024]{3,2,1,0:T(8,128)(2,1)S(1)} %bitcast.9) | data formatting | bytes 4194304

commit v3 on v2

v3 whole, which is shorter than its diff:
```python
import functools
import math

import jax
import jax.numpy as jnp
from jax import lax
from jax.experimental import pallas as pl
from jax.experimental.pallas import tpu as pltpu
from jax.sharding import PartitionSpec as P

HEADS = 28
KV_HEADS = 4
HEAD_DIM = 128
GROUP = HEADS // KV_HEADS
KVW = KV_HEADS * HEAD_DIM
PAD = 8
MESH = pl.DeviceIdType.MESH
BF16 = jnp.bfloat16
F32 = jnp.float32
CHUNKS = ((0, 256), (256, 256), (512, 384), (896, 128))
LAST = len(CHUNKS) - 1
TILE = 256


def lanes(index):
    return pl.ds(pl.multiple_of(index * HEAD_DIM, HEAD_DIM), HEAD_DIM)


def loop(start, stop, step):
    def run(i, carry):
        step(i)
        return carry

    lax.fori_loop(start, stop, run, 0)


def reshard_kernel(
    dims,
    len_ref, pm_hbm, pos_hbm, query_hbm, text_hbm, rows_hbm,
    place_ref, cache_ref, last_ref, own_w_ref, merge_ref,
    pm_ref, pos_ref, query_ref, text_ref, rows_ref,
    sort_ref, send_ref, got_ref, place_send, place_got,
    q_ref, score_ref, weight_ref, acc_ref, stat_ref, acc_got, stat_got,
    in_sems, send_sem, recv_sems, place_sem, xsend_sem, xstat_sem, xacc_sem,
):
    patches, seqs, reqs, layers, slot, band, text_dev = dims
    peers = patches * reqs
    msg = layers * slot
    total_rows = layers * band
    heads = layers * PAD
    patch, seq, req = (lax.axis_index(n) for n in ("patch", "seq", "req"))
    me = patch * reqs + req
    scale = 1.0 / math.sqrt(HEAD_DIM)

    def peer(step):
        other = me + step
        other = jnp.where(other >= peers, other - peers, other)
        return other, {"patch": other // reqs, "req": lax.rem(other, reqs)}

    def head_at(j):
        return lax.rem(seq + 1 + j, seqs)

    loads = [
        pltpu.make_async_copy(src, dst, in_sems.at[i])
        for i, (src, dst) in enumerate(
            (
                (pm_hbm, pm_ref),
                (rows_hbm, rows_ref),
                (pos_hbm, pos_ref),
                (query_hbm, query_ref),
                (text_hbm, text_ref),
            )
        )
    ]
    for i in range(3):
        loads[i].start()

    barrier = pltpu.get_barrier_semaphore()

    def greet(i):
        step = i + peers // 4
        _, device = peer(jnp.where(step >= peers, step - peers + 1, step))
        pl.semaphore_signal(barrier, inc=1, device_id=device, device_id_type=MESH)

    loop(0, peers - 1, greet)
    for step in range(1, seqs):
        pl.semaphore_signal(
            barrier, inc=1, device_id={"seq": lax.rem(seq + step, seqs)}, device_id_type=MESH
        )

    loads[0].wait()
    owner = pm_ref[...]
    member = lax.broadcasted_iota(jnp.int32, (peers, band), 0) == owner
    member_f = member.astype(F32)
    before = lax.broadcasted_iota(jnp.int32, (band, band), 0) < lax.broadcasted_iota(
        jnp.int32, (band, band), 1
    )
    counts = jnp.dot(
        member_f.astype(BF16), before.astype(F32).astype(BF16), preferred_element_type=F32
    )
    rank = jnp.sum(member_f * counts, axis=0, keepdims=True)
    target = owner.astype(F32) * msg + rank
    line = lax.broadcasted_iota(jnp.int32, (total_rows, band), 0).astype(F32)
    for l in range(layers):
        sort_ref[:, l * band : (l + 1) * band] = (
            (line == target + float(l * slot)).astype(F32).astype(BF16)
        )

    def sort_columns(source, start, width):
        def rows_of(i):
            lines = pl.ds(pl.multiple_of(i * TILE, TILE), TILE)
            send_ref[lines, start : start + width] = jnp.dot(
                sort_ref[lines, :], rows_ref[:, source], preferred_element_type=F32
            ).astype(BF16)

        loop(0, total_rows // TILE, rows_of)

    def sort_chunk(c):
        start, width = CHUNKS[c]
        if start < KVW:
            for j in range(start, start + width, TILE):
                sort_columns(slice(j, j + TILE), j, TILE)
        else:
            for j in range(start, start + width, HEAD_DIM):
                sort_columns(lanes(KV_HEADS + head_at((j - KVW) // HEAD_DIM)), j, HEAD_DIM)

    def arrivals(c):
        start, width = CHUNKS[c]
        return (last_ref, 0, width) if c == LAST else (got_ref, start, width)

    def block(ref, index, start, width):
        return ref.at[pl.ds(pl.multiple_of(index * msg, msg), msg), pl.ds(start, width)]

    def send_chunk(c):
        def send(step):
            other, device = peer(step)
            pltpu.make_async_remote_copy(
                src_ref=block(send_ref, other, *CHUNKS[c]),
                dst_ref=block(arrivals(c)[0], me, *arrivals(c)[1:]),
                send_sem=send_sem,
                recv_sem=recv_sems.at[c],
                device_id=device,
                device_id_type=MESH,
            ).start()

        loop(1, peers, send)

    loads[1].wait()
    sort_chunk(0)
    pl.semaphore_wait(barrier, peers - 1 + seqs - 1)
    send_chunk(0)
    loads[3].start()
    loads[4].start()

    loads[2].wait()
    local = pos_ref[...].astype(F32) - (seq * band).astype(F32)
    lane = lax.broadcasted_iota(jnp.int32, (peers, 128), 1)
    spread = ((lane // slot) % layers * band).astype(F32)
    for k in range(slot):
        mine = jnp.where(member & (counts == float(k)), local, 0.0)
        spread = spread + jnp.where(lane % slot == k, jnp.sum(mine, axis=1, keepdims=True), 0.0)
    place_send[...] = spread.reshape(peers, 1, 128)

    for c in range(1, LAST + 1):
        sort_chunk(c)
        send_chunk(c)
        if c == 1:

            def send_place(step):
                other, device = peer(step)
                pltpu.make_async_remote_copy(
                    src_ref=place_send.at[other],
                    dst_ref=place_got.at[me],
                    send_sem=send_sem,
                    recv_sem=place_sem,
                    device_id=device,
                    device_id_type=MESH,
                ).start()

            loop(1, peers, send_place)
    own = pl.ds(pl.multiple_of(me * msg, msg), msg)
    got_ref[own, :] = send_ref[own, : CHUNKS[LAST][0]]
    last_ref[own, :] = send_ref[own, CHUNKS[LAST][0] :]
    place_got[pl.ds(me, 1)] = place_send[pl.ds(me, 1)]

    loads[3].wait()
    q_ref[...] = jnp.zeros_like(q_ref)
    for l in range(layers):
        whole = query_ref[l : l + 1, :].astype(F32)
        for h in range(HEADS):
            g, k = divmod(h, GROUP)
            q_ref[g, l * PAD + k : l * PAD + k + 1, :] = whole[:, h * HEAD_DIM : (h + 1) * HEAD_DIM]

    loads[4].wait()
    length = len_ref[0]
    text_at = lax.broadcasted_iota(jnp.int32, (PAD, text_dev), 1) + seq * text_dev
    used = text_at < length

    def dot_t(a, b):
        return lax.dot_general(a, b, (((1,), (1,)), ((), ())), preferred_element_type=F32)

    for g in range(KV_HEADS):
        keys = slice(g * HEAD_DIM, (g + 1) * HEAD_DIM)
        for l in range(layers):
            lines = slice(l * PAD, (l + 1) * PAD)
            raw = dot_t(q_ref[g, lines, :].astype(BF16), text_ref[l, :, keys]) * scale
            score_ref[g, lines, :] = jnp.where(used, raw, -jnp.inf)

    def wait_all(sem, ref):
        pltpu.make_async_copy(ref, ref, sem).wait()

    def wait_chunk(c):
        ref, start, width = arrivals(c)
        wait_all(recv_sems.at[c], ref.at[pl.ds(0, (peers - 1) * msg), pl.ds(start, width)])

    wait_all(place_sem, place_got.at[pl.ds(0, peers - 1)])
    per_tile = 128 // msg
    first = lax.broadcasted_iota(jnp.int32, (per_tile, 128), 0)
    which = lax.broadcasted_iota(jnp.int32, (per_tile, 128), 1) // msg
    cache_line = lax.broadcasted_iota(jnp.int32, (total_rows, 128), 0).astype(F32)
    for b in range(peers // per_tile):
        tile = place_got[b * per_tile : (b + 1) * per_tile].reshape(per_tile, 128)
        to = jnp.sum(jnp.where(first == which, tile, 0.0), axis=0, keepdims=True)
        place_ref[:, b * 128 : (b + 1) * 128] = (cache_line == to).astype(F32).astype(BF16)

    def place_columns(start, width, to):
        def rows_of(i):
            lines = pl.ds(pl.multiple_of(i * TILE, TILE), TILE)
            cache_ref[lines, to] = jnp.dot(
                place_ref[lines, :], got_ref[:, start : start + width], preferred_element_type=F32
            ).astype(BF16)

        loop(0, total_rows // TILE, rows_of)

    def exchange(src_ref, dst_ref, j, sem):
        pltpu.make_async_remote_copy(
            src_ref=src_ref.at[head_at(j)],
            dst_ref=dst_ref.at[j],
            send_sem=xsend_sem,
            recv_sem=sem,
            device_id={"seq": head_at(j)},
            device_id_type=MESH,
        ).start()

    for c in (0, 1):
        wait_chunk(c)
    same_layer = (
        lax.broadcasted_iota(jnp.int32, (heads, total_rows), 1) // slot
    ) % layers == lax.broadcasted_iota(jnp.int32, (heads, total_rows), 0) // PAD
    half = lax.broadcasted_iota(jnp.int32, (heads, 128), 1) < 64
    for g in range(KV_HEADS):
        keys = slice(g * HEAD_DIM, (g + 1) * HEAD_DIM)
        vals = slice(KVW + g * HEAD_DIM, KVW + (g + 1) * HEAD_DIM)
        raw = dot_t(q_ref[g].astype(BF16), got_ref[:, keys]) * scale
        image = jnp.where(same_layer, raw, -jnp.inf)
        text = score_ref[g]
        top = jnp.maximum(
            jnp.max(image, axis=1, keepdims=True), jnp.max(text, axis=1, keepdims=True)
        )
        image_w = jnp.exp(image - top)
        text_w = jnp.exp(text - top)
        total = jnp.sum(image_w, axis=1, keepdims=True) + jnp.sum(text_w, axis=1, keepdims=True)
        weight_ref[g] = image_w.astype(BF16)
        stat_ref[g] = jnp.where(half, top, total)
        for l in range(layers):
            lines = slice(l * PAD, (l + 1) * PAD)
            acc_ref[g, lines, :] = jnp.dot(
                text_w[lines].astype(BF16), text_ref[l, :, vals], preferred_element_type=F32
            )
    for j in range(seqs - 1):
        exchange(stat_ref, stat_got, j, xstat_sem)
    own_w_ref[...] = weight_ref[seq]
    for j in range(0, KVW, TILE):
        place_columns(j, TILE, slice(j, j + TILE))

    wait_chunk(2)
    for j in range(seqs - 1):
        g = head_at(j)
        start = KVW + j * HEAD_DIM
        acc_ref[g] = acc_ref[g] + jnp.dot(
            weight_ref[g], got_ref[:, start : start + HEAD_DIM], preferred_element_type=F32
        )
    for j in range(seqs - 1):
        exchange(acc_ref, acc_got, j, xacc_sem)
    for j in range(seqs - 1):
        place_columns(KVW + j * HEAD_DIM, HEAD_DIM, lanes(KV_HEADS + head_at(j)))

    wait_all(xstat_sem, stat_got)
    stats = [stat_ref[seq]] + [stat_got[j] for j in range(seqs - 1)]
    top = functools.reduce(jnp.maximum, [s[:, 0:1] for s in stats])
    factors = [jnp.exp(s[:, 0:1] - top) for s in stats]
    total = sum(f * s[:, 64:65] for f, s in zip(factors, stats))
    wait_all(xacc_sem, acc_got)
    merge_ref[0] = factors[0] * acc_ref[seq] + sum(
        f * acc_got[j] for j, f in enumerate(factors[1:])
    )
    merge_ref[1] = jnp.broadcast_to(factors[0], (heads, HEAD_DIM))
    merge_ref[2] = jnp.broadcast_to(total, (heads, HEAD_DIM))

    for c in range(LAST):
        wait_all(
            send_sem, got_ref.at[pl.ds(0, (peers - 1) * msg), pl.ds(CHUNKS[c][0], CHUNKS[c][1])]
        )
    wait_all(send_sem, place_got.at[pl.ds(0, peers - 1)])
    wait_all(xsend_sem, stat_got)
    wait_all(xsend_sem, acc_got)
    wait_all(send_sem, last_ref.at[pl.ds(0, (peers - 1) * msg)])
    wait_chunk(LAST)


def finish_kernel(
    dims,
    place_ref, cache_ref, last_ref, own_w_ref, merge_ref,
    att_hbm, cache_hbm,
    att_ref, part_ref, sems,
):
    _, seqs, _, layers, _, band, _ = dims
    total_rows = layers * band
    seq = lax.axis_index("seq")
    copies = [pltpu.make_async_copy(cache_ref.at[:, :KVW], cache_hbm.at[:, :KVW], sems.at[0])]
    for j in range(seqs - 1):
        columns = lanes(KV_HEADS + lax.rem(seq + 1 + j, seqs))
        copies.append(
            pltpu.make_async_copy(
                cache_ref.at[:, columns], cache_hbm.at[:, columns], sems.at[1 + j]
            )
        )
    for copy in copies:
        copy.start()

    values = jnp.dot(own_w_ref[...], last_ref[...], preferred_element_type=F32)
    result = (merge_ref[0] + merge_ref[1] * values) / merge_ref[2]
    for l in range(layers):
        for k in range(GROUP):
            att_ref[l : l + 1, k * HEAD_DIM : (k + 1) * HEAD_DIM] = result[
                l * PAD + k : l * PAD + k + 1, :
            ].astype(BF16)
    copies.append(pltpu.make_async_copy(att_ref, att_hbm, sems.at[seqs]))
    copies[-1].start()

    columns = lanes(KV_HEADS + seq)
    for i in range(total_rows // TILE):
        lines = slice(i * TILE, (i + 1) * TILE)
        part_ref[lines, :] = jnp.dot(
            place_ref[lines, :], last_ref[...], preferred_element_type=F32
        ).astype(BF16)
        copies.append(
            pltpu.make_async_copy(
                part_ref.at[lines, :], cache_hbm.at[lines, columns], sems.at[seqs + 1 + i]
            )
        )
        copies[-1].start()
    for copy in copies:
        copy.wait()


def body(query, text_cache, text_len, image_rows, patch_map, image_places):
    layers = query.shape[0]
    text_dev = text_cache.shape[2]
    width = text_cache.shape[3]
    band = image_rows.shape[1]
    patches, seqs, reqs = (lax.axis_size(n) for n in ("patch", "seq", "req"))
    peers = patches * reqs
    slot = band // peers
    rows = layers * band
    heads = layers * PAD
    dims = (patches, seqs, reqs, layers, slot, band, text_dev)
    hbm = pl.BlockSpec(memory_space=pltpu.HBM)
    vmem = pl.BlockSpec(memory_space=pltpu.VMEM)
    parts = pl.pallas_call(
        functools.partial(reshard_kernel, dims),
        name="reshard",
        out_shape=(
            jax.ShapeDtypeStruct((rows, rows), BF16),
            jax.ShapeDtypeStruct((rows, width), BF16),
            jax.ShapeDtypeStruct((rows, HEAD_DIM), BF16),
            jax.ShapeDtypeStruct((heads, rows), BF16),
            jax.ShapeDtypeStruct((3, heads, HEAD_DIM), F32),
        ),
        in_specs=[pl.BlockSpec(memory_space=pltpu.SMEM)] + [hbm] * 5,
        out_specs=(vmem,) * 5,
        scratch_shapes=[
            pltpu.VMEM((1, band), jnp.int32),
            pltpu.VMEM((1, band), jnp.int32),
            pltpu.VMEM((layers, HEADS * HEAD_DIM), BF16),
            pltpu.VMEM((layers, text_dev, width), BF16),
            pltpu.VMEM((rows, width), BF16),
            pltpu.VMEM((rows, rows), BF16),
            pltpu.VMEM((rows, width), BF16),
            pltpu.VMEM((rows, width - HEAD_DIM), BF16),
            pltpu.VMEM((peers, 1, 128), F32),
            pltpu.VMEM((peers, 1, 128), F32),
            pltpu.VMEM((KV_HEADS, heads, HEAD_DIM), F32),
            pltpu.VMEM((KV_HEADS, heads, text_dev), F32),
            pltpu.VMEM((KV_HEADS, heads, rows), BF16),
            pltpu.VMEM((KV_HEADS, heads, HEAD_DIM), F32),
            pltpu.VMEM((KV_HEADS, heads, HEAD_DIM), F32),
            pltpu.VMEM((seqs - 1, heads, HEAD_DIM), F32),
            pltpu.VMEM((seqs - 1, heads, HEAD_DIM), F32),
            pltpu.SemaphoreType.DMA((5,)),
            pltpu.SemaphoreType.DMA,
            pltpu.SemaphoreType.DMA((len(CHUNKS),)),
            pltpu.SemaphoreType.DMA,
            pltpu.SemaphoreType.DMA,
            pltpu.SemaphoreType.DMA,
            pltpu.SemaphoreType.DMA,
        ],
        compiler_params=pltpu.CompilerParams(
            collective_id=0, has_side_effects=True, vmem_limit_bytes=48 * 1024 * 1024
        ),
    )(
        text_len,
        *(
            pltpu.with_memory_space_constraint(x, pltpu.HBM)
            for x in (
                patch_map.reshape(1, band),
                image_places.reshape(1, band),
                query.reshape(layers, HEADS * HEAD_DIM),
                text_cache.reshape(layers, text_dev, width),
                image_rows.reshape(rows, width),
            )
        ),
    )
    attended, cache = pl.pallas_call(
        functools.partial(finish_kernel, dims),
        name="finish",
        out_shape=(
            jax.ShapeDtypeStruct((layers, GROUP * HEAD_DIM), BF16),
            jax.ShapeDtypeStruct((rows, width), BF16),
        ),
        in_specs=[vmem] * 5,
        out_specs=(hbm, hbm),
        scratch_shapes=[
            pltpu.VMEM((layers, GROUP * HEAD_DIM), BF16),
            pltpu.VMEM((rows, HEAD_DIM), BF16),
            pltpu.SemaphoreType.DMA((seqs + 1 + rows // TILE,)),
        ],
        compiler_params=pltpu.CompilerParams(vmem_limit_bytes=16 * 1024 * 1024),
    )(*parts)
    return (
        attended.reshape(layers, 1, GROUP * HEAD_DIM),
        cache.reshape(layers, 1, band, width),
    )


def solution(mesh):
    return jax.shard_map(
        body,
        mesh=mesh,
        in_specs=(
            P(None, ("patch", "req"), None),
            P(None, ("patch", "req"), "seq", None),
            P(("patch", "req")),
            P(None, ("patch", "seq", "req"), None),
            P(("patch", "seq", "req")),
            P(("patch", "seq", "req")),
        ),
        out_specs=(P(None, ("patch", "req"), "seq"), P(None, ("patch", "req"), "seq", None)),
        check_vma=False,
    )
```

time: 66.1 us -> 62.4 us (0.944); the launches traced: 66.1 us -> 61.3 us
  Pallas kernels: 62.9 us -> 60 us
  local copies, waits for them, and re-layouts: 1.91 us -> 0 us
    pallas_call x1 -> x2, Pallas kernels: 62.9 us -> 60 us  [the longest x1 58.4 us: body(): pl.pallas_call(functools.partial(reshard_kernel, dims), name='reshard', o...]
    unnamed x2 -> x0, local copies, waits for them, and re-layouts: 1.91 us -> none
where the time goes in v3:
time: 62.4 us; the launch traced here: 61.3 us
  Pallas kernels  60 us (96%)
  between operations  1.28 us (2%)
    pallas_call x1, Pallas kernels, body(): pl.pallas_call(functools.partial(reshard_kernel, dims), name='reshard', o...  58.4 us
    pallas_call x1, Pallas kernels, body(): pl.pallas_call(functools.partial(finish_kernel, dims), name='finish', out...  1.58 us

profile of v3, /device:TPU:6, one launch (start us, length us, event | category | flops | bytes accessed | tf_op | source)
XLA Modules:
  0.0 61.3 jit_solution(2719462586046599798)
XLA Ops:
  1.3 58.4 %reshard.1 = (bf16[1024,1024]{1,0:T(8,128)(2,1)S(1)}, bf16[1024,1024]{1,0:T(8,128)(2,1)S(1)}, bf16[1024,128]{1,0:T(8,128)(2,1)S(1)}, bf16[32,1024]{1,0:T(8,128)(2,1)S(1)}, f32[3,32,128]{2,1,0:T(8,128)S(1)}) custom-call(s32[1]{0:T(128)S(6)} %copy.9.len_ref, s32[1,256]{1,0:T(1,128)} %bitcast.12, s32[1,256]{1,0:T(1,128)} %bitcast.13, bf16[4,3584]{1,0:T(4,128)(2,1)} %bitcast.11, ...), custom_call_target="tpu_custom_call" | custom-call | tf_op jit(solution)/shard_map/reshard/pallas_call | solution.py:370
  59.7 1.6 %finish.1 = (bf16[4,896]{1,0:T(4,128)(2,1)}, bf16[1024,1024]{1,0:T(8,128)(2,1)}) custom-call(bf16[1024,1024]{1,0:T(8,128)(2,1)S(1)} %get-tuple-element.9.place_ref, bf16[1024,1024]{1,0:T(8,128)(2,1)S(1)} %get-tuple-element.10.cache_ref, bf16[1024,128]{1,0:T(8,128)(2,1)S(1)} %get-tuple-element.11.last_ref, bf16[32,1024]{1,0:T(8,128)(2,1)S(1)} %get-tuple-element.12.own_w_ref, ...), custom_call_target="tpu_custom_call" | custom-call | tf_op jit(solution)/shard_map/finish/pallas_call | solution.py:424
